TPU v7x, 32 devices: a whole 2x2x4 slice. The times are simulated.
32 devices in a mesh: shard: 32 (over z, y, x, core).
Axes of the slice: x: 2, y: 2, z: 4, core: 2. Of those that a mesh axis runs over, the one named last changes fastest.
Arguments:
- data_t: bfloat16 [8192, 8192], P('shard'), may hold values from -0.125 to 0.125
- labels: int32 [8192], replicated, may hold values from -1 to 1, as said below
- sample_weight: float32 [8192], replicated, may hold values from 0.1 to 4
- w_start: float32 [8192], P('shard'), may hold values from -10 to 10
- alpha_start: float32 [8192], P('shard'), may hold values from 0 to 1
- visit_order: int32 [64, 128], P('shard'), may hold values from 0 to 127, each once within a row
Outputs:
- weights_out: float32 [8192], P('shard')
- alpha_final: float32 [8192], P('shard')
- objective: float32 [], replicated
Inputs may be any that keep to these rules, and one draw needn't show every extreme that they name: `labels`: each label is -1 or +1. `visit_order`: each row is a permutation of 0 to 127.
All inputs are finite; a program needn't handle non-finite values.
Results may differ from a plain program's by a relative error of at most 0.0047.
Values may be sent and summed in bfloat16 or wider, within the bound.
A program may use at most 64 MiB of HBM per device.

v0:
```python
import jax
import jax.numpy as jnp
from jax import lax
from jax.sharding import PartitionSpec as P

GROUP = 16


def sweep_rows(gram_block, label_rows, bound_rows, alpha_rows, margin_rows, visit_rows):
    gram_perm = gram_block[visit_rows][:, visit_rows]
    label_perm = label_rows[visit_rows]
    bound_perm = bound_rows[visit_rows]
    alpha_perm = alpha_rows[visit_rows]
    margin_perm = margin_rows[visit_rows]
    diag_perm = jnp.diagonal(gram_perm) + 1e-06

    def update_group(group_index, state_pair):
        alpha_now, margin_now = state_pair
        first_row = jnp.asarray(group_index * GROUP).astype(jnp.int32)
        group_alpha = lax.dynamic_slice_in_dim(alpha_now, first_row, GROUP)
        group_label = lax.dynamic_slice_in_dim(label_perm, first_row, GROUP)
        group_margin = lax.dynamic_slice_in_dim(margin_now, first_row, GROUP)
        group_diag = lax.dynamic_slice_in_dim(diag_perm, first_row, GROUP)
        group_bound = lax.dynamic_slice_in_dim(bound_perm, first_row, GROUP)
        fresh_alpha = jnp.clip(
            group_alpha + (1.0 - group_label * group_margin) / (2.0 * group_diag), 0.0, group_bound
        )
        change = fresh_alpha - group_alpha
        columns = lax.dynamic_slice_in_dim(gram_perm, first_row, GROUP, 1)
        margin_now = margin_now + 2.0 * jnp.dot(
            columns, group_label * change, precision=lax.Precision.HIGHEST
        )
        alpha_now = lax.dynamic_update_slice_in_dim(alpha_now, fresh_alpha, first_row, 0)
        return (alpha_now, margin_now)

    alpha_perm, margin_perm = lax.fori_loop(
        0, alpha_rows.shape[0] // GROUP, update_group, (alpha_perm, margin_perm)
    )
    return jnp.zeros_like(alpha_rows).at[visit_rows].set(alpha_perm)


def body(data_t, labels, sample_weight, w_start, alpha_start, visit_order):
    device_index = lax.axis_index("shard")
    devices = lax.axis_size("shard")
    local_feat = data_t.shape[0]
    samples = labels.shape[0]
    row_count = alpha_start.shape[0]
    features = local_feat * devices
    label_sign = labels.astype(jnp.float32)
    row_first = device_index * row_count
    own_signs = lax.dynamic_slice_in_dim(label_sign, row_first, row_count)
    own_bound = lax.dynamic_slice_in_dim(sample_weight, row_first, row_count)
    relaid = lax.all_to_all(data_t, "shard", split_axis=1, concat_axis=0, tiled=True)
    start_part = jnp.dot(w_start.astype(jnp.bfloat16), data_t, preferred_element_type=jnp.float32)
    start_margin = lax.psum(start_part, "shard")
    weighted = (
        sample_weight * label_sign * jnp.maximum(0.0, 1.0 - label_sign * start_margin)
    ).astype(jnp.bfloat16)
    ascent = jnp.dot(data_t, weighted, preferred_element_type=jnp.float32)
    column_sq = jnp.einsum("fs,fs->f", data_t, data_t, preferred_element_type=jnp.float32)
    scale_col = column_sq / samples + 1e-06
    stepped = w_start + ascent / (samples * scale_col)
    thresh = 1.0 / (4.0 * features * scale_col)
    primal = stepped - jnp.clip(stepped, -thresh, thresh)
    model_part = jnp.dot(primal.astype(jnp.bfloat16), data_t, preferred_element_type=jnp.float32)
    penalty_part = jnp.sum(jnp.abs(primal)) / (4.0 * features)
    own_margin = lax.psum_scatter(model_part, "shard", scatter_dimension=0, tiled=True)
    loss_part = jnp.sum(own_bound * jnp.square(jnp.maximum(0.0, 1.0 - own_signs * own_margin))) / (
        2.0 * samples
    )
    loss_total, penalty = lax.psum((loss_part, penalty_part), "shard")
    objective = loss_total + penalty
    gram_block = lax.dot_general(
        relaid, relaid, (((0,), (0,)), ((), ())), preferred_element_type=jnp.float32
    )
    block_count = visit_order.shape[0]
    visit_rows = (
        visit_order + (jnp.arange(block_count, dtype=jnp.int32) * visit_order.shape[1])[:, None]
    ).reshape(row_count)
    alpha_zero = own_bound * alpha_start
    alpha_one = sweep_rows(gram_block, own_signs, own_bound, alpha_zero, own_margin, visit_rows)
    change_one = (own_signs * (alpha_one - alpha_zero)).astype(jnp.bfloat16)
    update_part = jnp.dot(relaid, change_one, preferred_element_type=jnp.float32) * (2.0 / devices)
    update_one = lax.psum(update_part, "shard")
    second_margin = own_margin + jnp.dot(
        update_one.astype(jnp.bfloat16), relaid, preferred_element_type=jnp.float32
    )
    alpha_two = sweep_rows(gram_block, own_signs, own_bound, alpha_one, second_margin, visit_rows)
    change_two = (own_signs * (alpha_two - alpha_one)).astype(jnp.bfloat16)
    second_part = jnp.dot(relaid, change_two, preferred_element_type=jnp.float32) * (2.0 / devices)
    feat_first = device_index * local_feat
    update_two = lax.psum(second_part, "shard")
    own_two = lax.dynamic_slice_in_dim(update_two, feat_first, local_feat)
    own_one = lax.dynamic_slice_in_dim(update_one, feat_first, local_feat)
    return (primal + own_one + own_two, alpha_two, objective)


def solution(mesh):
    placed = (P("shard", None), P(), P(), P("shard"), P("shard"), P("shard", None))
    return jax.shard_map(
        body, mesh=mesh, in_specs=placed, out_specs=(P("shard"), P("shard"), P()), check_vma=False
    )
```

profile of v0, /device:TPU:14, one launch (start us, length us, event | category | flops | bytes accessed | tf_op | source)
XLA Modules:
  0.0 315.5 jit_solution(12440864550533348112)
XLA Ops:
  0.6 6.4 %copy.19 = bf16[256,8192]{0,1:T(8,128)(2,1)} copy(bf16[256,8192]{1,0:T(8,128)(2,1)} %param.10) | data formatting | bytes 8388608 | tf_op args[0]
  7.0 6.4 %copy.20 = bf16[256,32,256]{2,0,1:T(8,128)(2,1)} copy(bf16[256,32,256]{0,2,1:T(8,128)(2,1)} %bitcast.48) | data formatting | bytes 8388608 | tf_op jit(solution)/shard_map/all_to_all | solution.py:53
  13.4 6.0 %all-to-all-start = ((bf16[256,32,256]{2,0,1:T(8,128)(2,1)}), bf16[256,32,256]{2,0,1:T(8,128)(2,1)}, u32[]{:S(2)}, u32[]{:S(2)}) async-start(bf16[256,32,256]{2,0,1:T(8,128)(2,1)} %copy.20), calls=%async_computation | async-start | bytes 8388608 | tf_op jit(solution)/shard_map/all_to_all | solution.py:53
  19.5 2.8 fusion.28
  22.4 109.1 %psum.35 = f32[8192]{0:T(1024)S(1)} all-reduce(f32[8192]{0:T(1024)S(1)} %bitcast.53), channel_id=1, replica_groups=mesh['shard'=32] {'shard'}, use_global_device_ids=true, to_apply=%region_0.0 | all-reduce | flops 8192 | bytes 65536 | tf_op jit(solution)/shard_map/psum | solution.py:55
  131.5 3.5 %fusion.29 = f32[1,256]{1,0:T(1,128)S(1)} fusion(bf16[8192,1]{0,1:T(2,128)(2,1)S(1)} %reshape.137, bf16[256,8192]{1,0:T(8,128)(2,1)} %param.10), kind=kOutput, calls=%fused_computation.58 | convolution fusion | flops 4194304 | bytes 4211712 | tf_op jit(solution)/shard_map/dot_general | solution.py:59
  135.1 0.9 fusion.16
  136.0 0.6 abs_reduce_fusion
  136.6 2.8 fusion.30
  139.5 42.1 %all-reduce = f32[8192]{0:T(1024)S(1)} all-reduce(f32[8192]{0:T(1024)S(1)} %bitcast.54), channel_id=2, replica_groups=mesh['shard'=32] {'shard'}, use_global_device_ids=true, to_apply=%region_1.2.clone | all-reduce | flops 8192 | bytes 65536
  181.6 0.7 multiply_reduce_fusion
  182.3 1.9 gather_fusion.3
  184.3 1.9 gather_fusion.2
  186.3 1.9 gather_fusion
  188.2 1.9 gather_fusion.1
  191.5 4.7 %fusion.19 = f32[256,256]{1,0:T(8,128)S(1)} fusion(bf16[256,32,256]{2,0,1:T(8,128)(2,1)} %all-to-all-done), kind=kOutput, calls=%fused_computation.35 | convolution fusion | flops 1073741824 | bytes 4456448 | tf_op jit(solution)/shard_map/dot_general | solution.py:73
  196.2 1.0 gather_fusion.4
  197.3 1.0 gather_fusion.5
  198.5 2.4 gather_fusion.6
  200.8 8.5 %while.30 = (s32[]{:T(128)}, f32[256]{0:T(256)S(1)}, f32[256]{0:T(256)S(1)}, f32[256]{0:T(256)S(1)}, f32[256]{0:T(256)S(1)}, /*index=5*/f32[256]{0:T(256)S(1)}, ...) while((s32[]{:T(128)}, f32[256]{0:T(256)S(1)}, f32[256]{0:T(256)S(1)}, ...), condition=%wide.region_3.4_spmd, body=%wide.region_2.3_spmd.sunk | while | flops 49814 | bytes 145567 | solution.py:36
  201.1 0.2 fusion.57
  201.6 0.2 fusion.57
  202.1 0.2 fusion.57
  202.6 0.2 fusion.57
  203.2 0.2 fusion.57
  203.7 0.2 fusion.57
  204.2 0.2 fusion.57
  204.8 0.2 fusion.57
  205.3 0.2 fusion.57
  205.8 0.2 fusion.57
  206.4 0.2 fusion.57
  206.9 0.2 fusion.57
  207.4 0.2 fusion.57
  207.9 0.2 fusion.57
  208.5 0.2 fusion.57
  209.0 0.2 fusion.57
  209.3 1.4 scatter_custom_fusion
  210.7 1.9 gather_fusion.7
  212.7 3.4 %fusion.31 = f32[1,8192]{1,0:T(1,128)S(1)} fusion(bf16[256,1]{0,1:T(2,128)(2,1)S(1)} %reshape.144, bf16[8192,256]{1,0:T(8,128)(2,1)} %bitcast.14), kind=kOutput, calls=%fused_computation.60 | convolution fusion | flops 4194304 | bytes 4227584 | tf_op jit(solution)/shard_map/dot_general | solution.py:83
  216.1 38.4 %psum.36 = f32[8192]{0:T(1024)S(1)} all-reduce(f32[8192]{0:T(1024)S(1)} %broadcast_multiply_fusion.1), channel_id=1, replica_groups=mesh['shard'=32] {'shard'}, use_global_device_ids=true, to_apply=%region_5.6 | all-reduce | flops 8192 | bytes 65536 | tf_op jit(solution)/shard_map/psum | solution.py:84
  254.5 2.8 fusion.32
  257.4 2.0 gather_fusion.8
  259.3 8.5 %while.31 = (s32[]{:T(128)}, f32[256]{0:T(256)S(1)}, f32[256]{0:T(256)S(1)}, f32[256]{0:T(256)S(1)}, f32[256]{0:T(256)S(1)}, /*index=5*/f32[256]{0:T(256)S(1)}, ...) while((s32[]{:T(128)}, f32[256]{0:T(256)S(1)}, f32[256]{0:T(256)S(1)}, ...), condition=%wide.region_7.8_spmd, body=%wide.region_6.7_spmd.sunk | while | flops 49814 | bytes 145567 | solution.py:36
  259.5 0.2 fusion.61
  267.8 1.4 scatter_custom_fusion.1
  269.2 3.4 %fusion.33 = f32[1,8192]{1,0:T(1,128)S(1)} fusion(bf16[256,1]{0,1:T(2,128)(2,1)S(1)} %reshape.148, bf16[8192,256]{1,0:T(8,128)(2,1)} %bitcast.14), kind=kOutput, calls=%fused_computation.62 | convolution fusion | flops 4194304 | bytes 4227584 | tf_op jit(solution)/shard_map/dot_general | solution.py:90
  272.6 42.2 %all-reduce.1 = (f32[8192]{0:T(1024)S(1)}, f32[]{:T(128)}) all-reduce(f32[8192]{0:T(1024)S(1)} %broadcast_multiply_fusion, f32[]{:T(128)S(6)} %add.173), channel_id=1, replica_groups=mesh['shard'=32] {'shard'}, use_global_device_ids=true, to_apply=%region_9.10 | all-reduce | flops 8193 | bytes 65544 | tf_op jit(solution)/shard_map/psum | solution.py:92
  314.8 0.6 dynamic-slice_add_fusion
  (183 shorter events, 11.8 us)
Async XLA Ops:
  13.4 6.1 %copy-start.6 = (f32[256]{0:T(256)S(1)}, f32[256]{0:T(256)}, u32[]{:S(2)}) copy-start(f32[256]{0:T(256)} %param.13) | copy-start | bytes 3076
  13.4 6.1 %copy-start.1 = (s32[8192]{0:T(1024)S(1)}, s32[8192]{0:T(1024)}, u32[]{:S(2)}) copy-start(s32[8192]{0:T(1024)} %param.11) | copy-start | bytes 98308
  13.4 178.0 %all-to-all-start = ((bf16[256,32,256]{2,0,1:T(8,128)(2,1)}), bf16[256,32,256]{2,0,1:T(8,128)(2,1)}, u32[]{:S(2)}, u32[]{:S(2)}) async-start(bf16[256,32,256]{2,0,1:T(8,128)(2,1)} %copy.20), calls=%async_computation | async-start | bytes 8388608 | tf_op jit(solution)/shard_map/all_to_all | solution.py:53
  19.5 112.0 %copy-start.2 = (f32[8192]{0:T(1024)S(1)}, f32[8192]{0:T(1024)}, u32[]{:S(2)}) copy-start(f32[8192]{0:T(1024)} %param.12) | copy-start | bytes 98308
  131.5 3.6 %copy-start = (bf16[256,8192]{1,0:T(8,128)(2,1)S(1)}, bf16[256,8192]{1,0:T(8,128)(2,1)}, u32[]{:S(2)}) copy-start(bf16[256,8192]{1,0:T(8,128)(2,1)} %param.10) | copy-start | bytes 12582916
  135.1 47.2 %copy-start.5 = (s32[2,128]{1,0:T(2,128)S(1)}, s32[2,128]{1,0:T(2,128)}, u32[]{:S(2)}) copy-start(s32[2,128]{1,0:T(2,128)} %param.15) | copy-start | bytes 3076
  136.0 50.2 %copy-start.3 = (f32[256]{0:T(256)S(1)}, f32[256]{0:T(256)}, u32[]{:S(2)}) copy-start(f32[256]{0:T(256)} %param.14) | copy-start | bytes 3076
  269.2 46.3 %copy-start.4 = (f32[256]{0:T(256)}, f32[256]{0:T(256)S(1)}, u32[]{:S(2)}) copy-start(f32[256]{0:T(256)S(1)} %scatter_custom_fusion.1) | copy-start | bytes 3076
where the time goes:
time: 316 us; the launch traced here: 315 us
  blocking collectives  232 us (73%)
  local copies, waits for them, and re-layouts  32.1 us (10%)
  matrix products  31.5 us (10%)
  other arithmetic  10.4 us (3%)
  starting transfers between devices  6.02 us (2%)
    psum x1, blocking collectives, body(): start_margin = lax.psum(start_part, 'shard')  109 us
    psum x1, blocking collectives, body(): update_two = lax.psum(second_part, 'shard')  42.2 us
    unnamed x1, blocking collectives  42.1 us
    psum x1, blocking collectives, body(): update_one = lax.psum(update_part, 'shard')  38.4 us
    dot_general x32, matrix products, update_group(): jnp.dot(columns, group_label * change, precision=lax.Precision.HIGHEST)  7.97 us
    unnamed x15, local copies, waits for them, and re-layouts  6.44 us
    all_to_all x1, local copies, waits for them, and re-layouts, body(): lax.all_to_all(data_t, 'shard', split_axis=1, concat_axis=0, tiled=True)  6.41 us
  transfers between devices with their start and end apart: 1, of which 0 were waited for; matrix products, arithmetic and copies ran while one was open for 6% of the time, Pallas kernels for 0%

commit v1 on v0

--- a/solution.py
+++ b/solution.py
@@ -52,7 +52,11 @@
     own_bound = lax.dynamic_slice_in_dim(sample_weight, row_first, row_count)
     relaid = lax.all_to_all(data_t, "shard", split_axis=1, concat_axis=0, tiled=True)
     start_part = jnp.dot(w_start.astype(jnp.bfloat16), data_t, preferred_element_type=jnp.float32)
-    start_margin = lax.psum(start_part, "shard")
+    start_margin = start_part
+    for hop in (1, 2, 4, 8, 16):
+        start_margin = start_margin + lax.ppermute(
+            start_margin, "shard", [(dev, dev ^ hop) for dev in range(32)]
+        )
     weighted = (
         sample_weight * label_sign * jnp.maximum(0.0, 1.0 - label_sign * start_margin)
     ).astype(jnp.bfloat16)

time: 316 us -> 294 us (0.930)
  blocking collectives: 232 us -> 122 us
  waiting for transfers between devices: 0.01 us -> 80.8 us
  starting transfers between devices: 6.02 us -> 13.3 us
    psum x1 -> x0, blocking collectives: 109 us -> none  [body(): start_margin = lax.psum(start_part, 'shard')]
    ppermute x0 -> x5, waiting for transfers between devices: none -> 80.8 us  [body(): lax.ppermute(start_margin, 'shard', [(dev, dev ^ hop) for dev in range(32)])]
    ppermute x0 -> x5, starting transfers between devices: none -> 7.26 us  [body(): lax.ppermute(start_margin, 'shard', [(dev, dev ^ hop) for dev in range(32)])]
    unnamed x15 -> x17, local copies, waits for them, and re-layouts: 6.44 us -> 6.7 us
  transfers between devices with their start and end apart: 1 -> 6, of which waited for: 0 -> 4; matrix products, arithmetic and copies ran while one was open for 6% -> 6% of each run, Pallas kernels for 0% -> 0%
where the time goes in v1:
time: 294 us; the launch traced here: 292 us
  blocking collectives  122 us (41%)
  waiting for transfers between devices  80.8 us (27%)
  local copies, waits for them, and re-layouts  32.4 us (11%)
  matrix products  29.3 us (10%)
  starting transfers between devices  13.3 us (5%)
  other arithmetic  10.4 us (4%)
    ppermute x5, waiting for transfers between devices, body(): lax.ppermute(start_margin, 'shard', [(dev, dev ^ hop) for dev in range(32)])  80.8 us
    unnamed x1, blocking collectives  41.4 us
    psum x1, blocking collectives, body(): update_two = lax.psum(second_part, 'shard')  40.7 us
    psum x1, blocking collectives, body(): update_one = lax.psum(update_part, 'shard')  39.9 us
    dot_general x32, matrix products, update_group(): jnp.dot(columns, group_label * change, precision=lax.Precision.HIGHEST)  7.97 us
    ppermute x5, starting transfers between devices, body(): lax.ppermute(start_margin, 'shard', [(dev, dev ^ hop) for dev in range(32)])  7.26 us
    unnamed x17, local copies, waits for them, and re-layouts  6.7 us
    all_to_all x1, local copies, waits for them, and re-layouts, body(): lax.all_to_all(data_t, 'shard', split_axis=1, concat_axis=0, tiled=True)  6.48 us
  transfers between devices with their start and end apart: 6, of which 4 were waited for; matrix products, arithmetic and copies ran while one was open for 6% of the time, Pallas kernels for 0%

profile of v1, /device:TPU:14, one launch (start us, length us, event | category | flops | bytes accessed | tf_op | source)
XLA Modules:
  0.0 291.9 jit_solution(1930721526632924787)
XLA Ops:
  0.6 6.4 %copy.19 = bf16[256,8192]{0,1:T(8,128)(2,1)} copy(bf16[256,8192]{1,0:T(8,128)(2,1)} %param.10) | data formatting | bytes 8388608 | tf_op args[0]
  7.0 6.5 %copy.20 = bf16[256,32,256]{2,0,1:T(8,128)(2,1)} copy(bf16[256,32,256]{0,2,1:T(8,128)(2,1)} %bitcast.48) | data formatting | bytes 8388608 | tf_op jit(solution)/shard_map/all_to_all | solution.py:53
  13.5 6.0 %all-to-all-start = ((bf16[256,32,256]{2,0,1:T(8,128)(2,1)}), bf16[256,32,256]{2,0,1:T(8,128)(2,1)}, u32[]{:S(2)}, u32[]{:S(2)}) async-start(bf16[256,32,256]{2,0,1:T(8,128)(2,1)} %copy.20), calls=%async_computation | async-start | bytes 8388608 | tf_op jit(solution)/shard_map/all_to_all | solution.py:53
  19.6 3.0 %fusion.28 = f32[1,8192]{1,0:T(1,128)S(1)} fusion(bf16[256,1]{0,1:T(2,128)(2,1)S(1)} %reshape.135, bf16[256,8192]{1,0:T(8,128)(2,1)} %param.10), kind=kOutput, calls=%fused_computation.57 | convolution fusion | flops 4194304 | bytes 4227584 | tf_op jit(solution)/shard_map/dot_general | solution.py:54
  22.7 0.3 copy-done
  23.0 0.9 fusion.16
  23.9 0.6 collective-permute-start.1
  24.6 20.9 %collective-permute-done.1 = f32[8192]{0:T(1024)S(1)} collective-permute-done((f32[8192]{0:T(1024)S(1)}, f32[8192]{0:T(1024)S(1)}, u32[]{:S(2)}, u32[]{:S(2)}) %collective-permute-start.1) | collective-permute-done | bytes 32800 | tf_op jit(solution)/shard_map/ppermute | solution.py:57
  45.5 3.9 %collective-permute-done.2 = f32[8192]{0:T(1024)S(1)} collective-permute-done((f32[8192]{0:T(1024)S(1)}, f32[8192]{0:T(1024)S(1)}, u32[]{:S(2)}, u32[]{:S(2)}) %collective-permute-start.2) | collective-permute-done | bytes 32800 | tf_op jit(solution)/shard_map/ppermute | solution.py:57
  49.4 5.6 %collective-permute-start.3 = (f32[8192]{0:T(1024)S(1)}, f32[8192]{0:T(1024)S(1)}, u32[]{:S(2)}, u32[]{:S(2)}) collective-permute-start(f32[8192]{0:T(1024)S(1)} %add.178), channel_id=1, source_target_pairs={{0,8},{1,9},{2,10},{3,11},{4,12},{5,13},{6,14},{7,15},{8,0},{9,1},... | collective-permute-start | bytes 98312 | tf_op jit(solution)/shard_map/ppermute | solution.py:57
  55.1 35.2 %collective-permute-done.3 = f32[8192]{0:T(1024)S(1)} collective-permute-done((f32[8192]{0:T(1024)S(1)}, f32[8192]{0:T(1024)S(1)}, u32[]{:S(2)}, u32[]{:S(2)}) %collective-permute-start.3) | collective-permute-done | bytes 32800 | tf_op jit(solution)/shard_map/ppermute | solution.py:57
  90.3 0.9 collective-permute-start.4
  91.2 20.8 %collective-permute-done.4 = f32[8192]{0:T(1024)S(1)} collective-permute-done((f32[8192]{0:T(1024)S(1)}, f32[8192]{0:T(1024)S(1)}, u32[]{:S(2)}, u32[]{:S(2)}) %collective-permute-start.4) | collective-permute-done | bytes 32800 | tf_op jit(solution)/shard_map/ppermute | solution.py:57
  112.0 3.4 %fusion.29 = f32[1,256]{1,0:T(1,128)S(1)} fusion(bf16[8192,1]{0,1:T(2,128)(2,1)S(1)} %reshape.137, bf16[256,8192]{1,0:T(8,128)(2,1)} %param.10), kind=kOutput, calls=%fused_computation.58 | convolution fusion | flops 4194304 | bytes 4211712 | tf_op jit(solution)/shard_map/dot_general | solution.py:63
  115.4 0.6 abs_reduce_fusion
  116.1 0.7 fusion.30
  116.7 41.4 %all-reduce = f32[8192]{0:T(1024)S(1)} all-reduce(f32[8192]{0:T(1024)S(1)} %bitcast.55), channel_id=2, replica_groups=mesh['shard'=32] {'shard'}, use_global_device_ids=true, to_apply=%region_0.1.clone | all-reduce | flops 8192 | bytes 65536
  158.1 0.7 multiply_reduce_fusion
  158.8 1.9 gather_fusion.3
  160.7 1.9 gather_fusion.2
  162.7 1.9 gather_fusion
  164.7 1.9 gather_fusion.1
  167.9 4.7 %fusion.19 = f32[256,256]{1,0:T(8,128)S(1)} fusion(bf16[256,32,256]{2,0,1:T(8,128)(2,1)} %all-to-all-done), kind=kOutput, calls=%fused_computation.35 | convolution fusion | flops 1073741824 | bytes 4456448 | tf_op jit(solution)/shard_map/dot_general | solution.py:77
  172.7 1.0 gather_fusion.4
  173.8 1.0 gather_fusion.5
  174.9 2.4 gather_fusion.6
  177.3 8.5 %while.30 = (s32[]{:T(128)}, f32[256]{0:T(256)S(1)}, f32[256]{0:T(256)S(1)}, f32[256]{0:T(256)S(1)}, f32[256]{0:T(256)S(1)}, /*index=5*/f32[256]{0:T(256)S(1)}, ...) while((s32[]{:T(128)}, f32[256]{0:T(256)S(1)}, f32[256]{0:T(256)S(1)}, ...), condition=%wide.region_2.3_spmd, body=%wide.region_1.2_spmd.sunk | while | flops 49814 | bytes 145567 | solution.py:36
  177.5 0.2 fusion.57
  178.0 0.2 fusion.57
  178.6 0.2 fusion.57
  179.1 0.2 fusion.57
  179.6 0.2 fusion.57
  180.1 0.2 fusion.57
  180.7 0.2 fusion.57
  181.2 0.2 fusion.57
  181.7 0.2 fusion.57
  182.3 0.2 fusion.57
  185.8 1.4 scatter_custom_fusion
  187.2 1.9 gather_fusion.7
  189.2 3.4 %fusion.31 = f32[1,8192]{1,0:T(1,128)S(1)} fusion(bf16[256,1]{0,1:T(2,128)(2,1)S(1)} %reshape.144, bf16[8192,256]{1,0:T(8,128)(2,1)} %bitcast.14), kind=kOutput, calls=%fused_computation.60 | convolution fusion | flops 4194304 | bytes 4227584 | tf_op jit(solution)/shard_map/dot_general | solution.py:87
  192.5 39.9 %psum.28 = f32[8192]{0:T(1024)S(1)} all-reduce(f32[8192]{0:T(1024)S(1)} %broadcast_multiply_fusion.1), channel_id=1, replica_groups=mesh['shard'=32] {'shard'}, use_global_device_ids=true, to_apply=%region_4.5 | all-reduce | flops 8192 | bytes 65536 | tf_op jit(solution)/shard_map/psum | solution.py:88
  232.5 2.8 fusion.32
  235.3 2.0 gather_fusion.8
  237.3 8.5 %while.31 = (s32[]{:T(128)}, f32[256]{0:T(256)S(1)}, f32[256]{0:T(256)S(1)}, f32[256]{0:T(256)S(1)}, f32[256]{0:T(256)S(1)}, /*index=5*/f32[256]{0:T(256)S(1)}, ...) while((s32[]{:T(128)}, f32[256]{0:T(256)S(1)}, f32[256]{0:T(256)S(1)}, ...), condition=%wide.region_6.7_spmd, body=%wide.region_5.6_spmd.sunk | while | flops 49814 | bytes 145567 | solution.py:36
  245.8 1.4 scatter_custom_fusion.1
  247.2 3.4 %fusion.33 = f32[1,8192]{1,0:T(1,128)S(1)} fusion(bf16[256,1]{0,1:T(2,128)(2,1)S(1)} %reshape.148, bf16[8192,256]{1,0:T(8,128)(2,1)} %bitcast.14), kind=kOutput, calls=%fused_computation.62 | convolution fusion | flops 4194304 | bytes 4227584 | tf_op jit(solution)/shard_map/dot_general | solution.py:94
  250.6 40.7 %all-reduce.1 = (f32[8192]{0:T(1024)S(1)}, f32[]{:T(128)}) all-reduce(f32[8192]{0:T(1024)S(1)} %broadcast_multiply_fusion, f32[]{:T(128)S(6)} %add.191), channel_id=1, replica_groups=mesh['shard'=32] {'shard'}, use_global_device_ids=true, to_apply=%region_8.9 | all-reduce | flops 8193 | bytes 65544 | tf_op jit(solution)/shard_map/psum | solution.py:96
  291.3 0.6 dynamic-slice_add_fusion
  (198 shorter events, 13.7 us)
Async XLA Ops:
  13.5 6.0 %copy-start.7 = (f32[256]{0:T(256)S(1)}, f32[256]{0:T(256)}, u32[]{:S(2)}) copy-start(f32[256]{0:T(256)} %param.13) | copy-start | bytes 3076
  13.5 154.4 %all-to-all-start = ((bf16[256,32,256]{2,0,1:T(8,128)(2,1)}), bf16[256,32,256]{2,0,1:T(8,128)(2,1)}, u32[]{:S(2)}, u32[]{:S(2)}) async-start(bf16[256,32,256]{2,0,1:T(8,128)(2,1)} %copy.20), calls=%async_computation | async-start | bytes 8388608 | tf_op jit(solution)/shard_map/all_to_all | solution.py:53
  19.5 3.5 %copy-start = (bf16[256,8192]{1,0:T(8,128)(2,1)S(1)}, bf16[256,8192]{1,0:T(8,128)(2,1)}, u32[]{:S(2)}) copy-start(bf16[256,8192]{1,0:T(8,128)(2,1)} %param.10) | copy-start | bytes 12582916
  19.6 5.0 %copy-start.6 = (s32[2,128]{1,0:T(2,128)S(1)}, s32[2,128]{1,0:T(2,128)}, u32[]{:S(2)}) copy-start(s32[2,128]{1,0:T(2,128)} %param.15) | copy-start | bytes 3076
  19.6 71.6 %copy-start.2 = (s32[8192]{0:T(1024)S(1)}, s32[8192]{0:T(1024)}, u32[]{:S(2)}) copy-start(s32[8192]{0:T(1024)} %param.11) | copy-start | bytes 98308
  19.6 92.4 %copy-start.3 = (f32[8192]{0:T(1024)S(1)}, f32[8192]{0:T(1024)}, u32[]{:S(2)}) copy-start(f32[8192]{0:T(1024)} %param.12) | copy-start | bytes 98308
  22.6 1.3 collective-permute-start
  23.9 21.6 %collective-permute-start.1 = (f32[8192]{0:T(1024)S(1)}, f32[8192]{0:T(1024)S(1)}, u32[]{:S(2)}, u32[]{:S(2)}) collective-permute-start(f32[8192]{0:T(1024)S(1)} %add.176), channel_id=1, source_target_pairs={{0,2},{1,3},{2,0},{3,1},{4,6},{5,7},{6,4},{7,5},{8,10},{9,11},{10,... | collective-permute-start | bytes 98312 | tf_op jit(solution)/shard_map/ppermute | solution.py:57
  45.5 3.9 %collective-permute-start.2 = (f32[8192]{0:T(1024)S(1)}, f32[8192]{0:T(1024)S(1)}, u32[]{:S(2)}, u32[]{:S(2)}) collective-permute-start(f32[8192]{0:T(1024)S(1)} %add.177), channel_id=1, source_target_pairs={{0,4},{1,5},{2,6},{3,7},{4,0},{5,1},{6,2},{7,3},{8,12},{9,13},{10,... | collective-permute-start | bytes 98312 | tf_op jit(solution)/shard_map/ppermute | solution.py:57
  49.4 40.9 %collective-permute-start.3 = (f32[8192]{0:T(1024)S(1)}, f32[8192]{0:T(1024)S(1)}, u32[]{:S(2)}, u32[]{:S(2)}) collective-permute-start(f32[8192]{0:T(1024)S(1)} %add.178), channel_id=1, source_target_pairs={{0,8},{1,9},{2,10},{3,11},{4,12},{5,13},{6,14},{7,15},{8,0},{9,1},... | collective-permute-start | bytes 98312 | tf_op jit(solution)/shard_map/ppermute | solution.py:57
  90.3 21.7 %collective-permute-start.4 = (f32[8192]{0:T(1024)S(1)}, f32[8192]{0:T(1024)S(1)}, u32[]{:S(2)}, u32[]{:S(2)}) collective-permute-start(f32[8192]{0:T(1024)S(1)} %add.179), channel_id=1, source_target_pairs={{0,16},{1,17},{2,18},{3,19},{4,20},{5,21},{6,22},{7,23},{8,24},{9,... | collective-permute-start | bytes 98312 | tf_op jit(solution)/shard_map/ppermute | solution.py:57
  91.2 24.8 %copy-start.1 = (bf16[256,8192]{1,0:T(8,128)(2,1)S(1)}, bf16[256,8192]{1,0:T(8,128)(2,1)}, u32[]{:S(2)}) copy-start(bf16[256,8192]{1,0:T(8,128)(2,1)} %param.10) | copy-start | bytes 12582916
  115.4 47.3 %copy-start.4 = (f32[256]{0:T(256)S(1)}, f32[256]{0:T(256)}, u32[]{:S(2)}) copy-start(f32[256]{0:T(256)} %param.14) | copy-start | bytes 3076
  247.2 44.8 %copy-start.5 = (f32[256]{0:T(256)}, f32[256]{0:T(256)S(1)}, u32[]{:S(2)}) copy-start(f32[256]{0:T(256)S(1)} %scatter_custom_fusion.1) | copy-start | bytes 3076
